TPU v7x, 32 devices: a whole 2x2x4 slice. The times are simulated.
32 devices in a mesh: gx: 4 (over y, core), gy: 4 (over z), gz: 2 (over x).
Axes of the slice: x: 2, y: 2, z: 4, core: 2. Of those that a mesh axis runs over, the one named last changes fastest.
Arguments:
- residual: float32 [32, 128, 256], P('gx', 'gy', 'gz'), may hold values from -32 to 32
- direction: float32 [32, 128, 256], P('gx', 'gy', 'gz'), may hold values from -32 to 32
- diagonal: float32 [32, 128, 256], P('gx', 'gy', 'gz'), may hold values from 0.5 to 2
- recycled: bfloat16 [16, 32, 128, 256], P(None, 'gx', 'gy', 'gz'), may hold values from -6 to 6
- recycled_images: bfloat16 [16, 32, 128, 256], P(None, 'gx', 'gy', 'gz'), may hold values from -0.0014648438 to 0.0014648438
- coupling_inverse: float32 [16, 16], replicated, may hold values from -1 to 3, as said below
Outputs:
- solution_delta: float32 [32, 128, 256], P('gx', 'gy', 'gz')
- new_residual: float32 [32, 128, 256], P('gx', 'gy', 'gz')
- new_direction: float32 [32, 128, 256], P('gx', 'gy', 'gz')
Inputs may be any that keep to these rules, and one draw needn't show every extreme that they name: `coupling_inverse`: symmetric.
All inputs are finite; a program needn't handle non-finite values.
Results may differ from a plain program's by a relative error of at most 0.0028.
Values sent between devices are 32-bit elements; how exact they have to be, the bound alone decides.
No kernel may reach another device: no remote copies, remote signals or barrier semaphores. Data moves between devices by JAX's collectives and lax.ppermute only.
A program may use at most 64 MiB of HBM per device.

v0:
```python
import jax
import jax.numpy as jnp
import numpy as np
from jax import lax
from jax.sharding import PartitionSpec as P

S = 4
BASIS = 9
center = 7.25
half_width = 6.75


def extended(block, sides, width):
    for axis, dim in sides:
        count = lax.axis_size(axis)
        forward = [(i, i + 1) for i in range(count - 1)]
        forward.append((count - 1, 0))
        backward = [(target, source) for source, target in forward]
        low = lax.ppermute(
            lax.slice_in_dim(block, block.shape[dim] - width, None, axis=dim), axis, forward
        )
        high = lax.ppermute(lax.slice_in_dim(block, 0, width, axis=dim), axis, backward)
        block = jnp.concatenate([low, block, high], axis=dim)
    return block


def inside(padded):
    centre_cells = padded[:, 1:-1, 1:-1, 1:-1]
    beside_all = padded[:, 2:, 1:-1, 1:-1] + padded[:, :-2, 1:-1, 1:-1]
    beside_all = beside_all + padded[:, 1:-1, 2:, 1:-1] + padded[:, 1:-1, :-2, 1:-1]
    beside_all = beside_all + padded[:, 1:-1, 1:-1, 2:] + padded[:, 1:-1, 1:-1, :-2]
    return (centre_cells, beside_all)


def trim_margin(values, margin):
    if margin == 0:
        return values
    return values[..., margin:-margin, margin:-margin, margin:-margin]


def chebyshev_next(current, beside_all, diagonal, earlier):
    mapped = (6.0 + diagonal) * current - beside_all
    scaled = (mapped - center * current) / half_width
    if earlier is None:
        return scaled
    return 2.0 * scaled - earlier


def recurrence_matrix():
    recurrence = np.zeros((BASIS, BASIS), np.float32)
    for offset, length in ((0, S + 1), (S + 1, S)):
        recurrence[offset, offset] = center
        recurrence[offset + 1, offset] = half_width
        for column in range(1, length - 1):
            recurrence[offset + column + 1, offset + column] = half_width / 2
            recurrence[offset + column, offset + column] = center
            recurrence[offset + column - 1, offset + column] = half_width / 2
    return jnp.asarray(recurrence, dtype=jnp.float32)


def coordinates(totals, coupling_inverse):
    precise = lax.Precision.HIGHEST
    gram_block = totals[:BASIS]
    projections = totals[BASIS:]
    recurrence = recurrence_matrix()
    counter = jnp.arange(BASIS)
    residue = (counter == S + 1).astype(jnp.float32)
    search = (counter == 0).astype(jnp.float32)
    update = jnp.zeros((BASIS,), jnp.float32)
    norm_now = jnp.dot(residue, jnp.dot(gram_block, residue, precision=precise), precision=precise)
    for iteration in range(S):
        mapped = jnp.dot(recurrence, search, precision=precise)
        step_size = norm_now / jnp.dot(
            search, jnp.dot(gram_block, mapped, precision=precise), precision=precise
        )
        update = update + step_size * search
        residue = residue - step_size * mapped
        norm_next = jnp.dot(
            residue, jnp.dot(gram_block, residue, precision=precise), precision=precise
        )
        search = residue + norm_next / norm_now * search
        norm_now = norm_next
    weights = jnp.dot(
        coupling_inverse, jnp.dot(projections, residue, precision=precise), precision=precise
    )
    return (update, residue, search, weights.astype(jnp.bfloat16))


def body(residual, direction, diagonal, recycled, recycled_images, coupling_inverse):
    precise = lax.Precision.HIGHEST
    search_basis = [direction]
    residue_basis = [residual]
    earlier = None
    packed = jnp.stack([direction, residual, diagonal])
    padded = extended(packed, (("gx", 1), ("gy", 2), ("gz", 3)), S)
    wide_diag = padded[2]
    current = padded[:2]
    for iteration in range(S):
        if iteration == S - 1:
            current = current[:1]
            earlier = earlier[:1]
        centre_cells, beside_all = inside(current)
        margin = S - iteration - 1
        local_diag = trim_margin(wide_diag, iteration + 1)
        previous = None if earlier is None else trim_margin(earlier, 2)
        following = chebyshev_next(centre_cells, beside_all, local_diag, previous)
        earlier, current = (current, following)
        search_basis.append(trim_margin(following[0], margin))
        if following.shape[0] > 1:
            residue_basis.append(trim_margin(following[1], margin))
    basis = jnp.stack(search_basis + residue_basis)
    basis_flat = basis.reshape(basis.shape[0], -1)
    gram_block = lax.dot_general(
        basis_flat,
        basis_flat,
        (((1,), (1,)), ((), ())),
        precision=precise,
        preferred_element_type=jnp.float32,
    )
    rounded = basis_flat.astype(jnp.bfloat16)
    images = recycled_images.reshape(recycled_images.shape[0], -1)
    projections = lax.dot_general(
        images, rounded, (((1,), (1,)), ((), ())), preferred_element_type=jnp.float32
    )
    totals = lax.psum(jnp.concatenate([gram_block, projections], 0), ("gx", "gy", "gz"))
    update, residue, search, weights = coordinates(totals, coupling_inverse)
    shape = residual.shape
    solution_delta = jnp.dot(update, basis_flat, precision=precise).reshape(shape)
    new_residual = jnp.dot(residue, basis_flat, precision=precise).reshape(shape)
    correction = jnp.dot(
        weights, recycled.reshape(recycled.shape[0], -1), preferred_element_type=jnp.float32
    )
    new_direction = (jnp.dot(search, basis_flat, precision=precise) - correction).reshape(shape)
    return (solution_delta, new_residual, new_direction)


def solution(mesh):
    in_specs = (
        P("gx", "gy", "gz"),
        P("gx", "gy", "gz"),
        P("gx", "gy", "gz"),
        P(None, "gx", "gy", "gz"),
        P(None, "gx", "gy", "gz"),
        P(),
    )
    out_specs = (P("gx", "gy", "gz"), P("gx", "gy", "gz"), P("gx", "gy", "gz"))
    return jax.shard_map(body, mesh=mesh, in_specs=in_specs, out_specs=out_specs, check_vma=False)
```

profile of v0, /device:TPU:0, one launch (start us, length us, event | category | flops | bytes accessed | tf_op | source)
XLA Modules:
  0.0 110.9 jit_solution(13209403578807758797)
XLA Ops:
  0.7 1.1 %pad_maximum_fusion.2 = f32[3,8,32,128]{3,2,1,0:T(8,128)S(1)} fusion(f32[1,8,32,128]{3,2,1,0:T(8,128)} %bitcast.257, f32[1,8,32,128]{3,2,1,0:T(8,128)} %bitcast.251, f32[1,8,32,128]{3,2,1,0:T(8,128)} %bitcast.245), kind=kLoop, calls=%fused_computation.81 | loop fusion | flops 196608 | bytes 786432 | tf_op jit(solution)/shard_map/stack | solution.py:94
  2.4 2.0 %collective-permute-start.1 = (f32[3,4,32,128]{3,2,1,0:T(8,128)S(1)}, f32[3,4,32,128]{3,2,1,0:T(8,128)S(1)}, u32[]{:S(2)}, u32[]{:S(2)}) collective-permute-start(f32[3,4,32,128]{3,2,1,0:T(8,128)S(1)} %get-tuple-element.14), channel_id=1, source_target_pairs={{8,0},{16,8},{24,16},{0,24},{9,1},{17,9},{25,17},{1,25},{10,2},{18... | collective-permute-start | bytes 589832 | tf_op jit(solution)/shard_map/ppermute | solution.py:22
  4.4 3.3 %collective-permute-done = f32[3,4,32,128]{3,2,1,0:T(8,128)S(1)} collective-permute-done((f32[3,4,32,128]{3,2,1,0:T(8,128)S(1)}, f32[3,4,32,128]{3,2,1,0:T(8,128)S(1)}, u32[]{:S(2)}, u32[]{:S(2)}) %collective-permute-start) | collective-permute-done | bytes 196640 | tf_op jit(solution)/shard_map/ppermute | solution.py:19
  7.7 1.9 %collective-permute-done.1 = f32[3,4,32,128]{3,2,1,0:T(8,128)S(1)} collective-permute-done((f32[3,4,32,128]{3,2,1,0:T(8,128)S(1)}, f32[3,4,32,128]{3,2,1,0:T(8,128)S(1)}, u32[]{:S(2)}, u32[]{:S(2)}) %collective-permute-start.1) | collective-permute-done | bytes 196640 | tf_op jit(solution)/shard_map/ppermute | solution.py:22
  9.6 0.9 pad_maximum_fusion.7
  10.5 1.6 %collective-permute-start.2 = (f32[3,16,4,128]{3,2,1,0:T(4,128)S(1)}, f32[3,16,4,128]{3,2,1,0:T(4,128)S(1)}, u32[]{:S(2)}, u32[]{:S(2)}) collective-permute-start(f32[3,16,4,128]{3,2,1,0:T(4,128)S(1)} %get-tuple-element.11), channel_id=1, source_target_pairs={{0,2},{2,4},{4,6},{6,0},{1,3},{3,5},{5,7},{7,1},{8,10},{10,12},{12... | collective-permute-start | bytes 294920 | tf_op jit(solution)/shard_map/ppermute | solution.py:19
  12.1 2.2 %collective-permute-start.3 = (f32[3,16,4,128]{3,2,1,0:T(4,128)S(1)}, f32[3,16,4,128]{3,2,1,0:T(4,128)S(1)}, u32[]{:S(2)}, u32[]{:S(2)}) collective-permute-start(f32[3,16,4,128]{3,2,1,0:T(4,128)S(1)} %get-tuple-element.12), channel_id=1, source_target_pairs={{2,0},{4,2},{6,4},{0,6},{3,1},{5,3},{7,5},{1,7},{10,8},{12,10},{14... | collective-permute-start | bytes 294920 | tf_op jit(solution)/shard_map/ppermute | solution.py:22
  14.4 3.7 %collective-permute-done.2 = f32[3,16,4,128]{3,2,1,0:T(4,128)S(1)} collective-permute-done((f32[3,16,4,128]{3,2,1,0:T(4,128)S(1)}, f32[3,16,4,128]{3,2,1,0:T(4,128)S(1)}, u32[]{:S(2)}, u32[]{:S(2)}) %collective-permute-start.2) | collective-permute-done | bytes 98336 | tf_op jit(solution)/shard_map/ppermute | solution.py:19
  18.0 1.4 %collective-permute-done.3 = f32[3,16,4,128]{3,2,1,0:T(4,128)S(1)} collective-permute-done((f32[3,16,4,128]{3,2,1,0:T(4,128)S(1)}, f32[3,16,4,128]{3,2,1,0:T(4,128)S(1)}, u32[]{:S(2)}, u32[]{:S(2)}) %collective-permute-start.3) | collective-permute-done | bytes 98336 | tf_op jit(solution)/shard_map/ppermute | solution.py:22
  20.3 1.6 %collective-permute-start.4 = (f32[3,16,40,4]{2,1,3,0:T(8,128)S(1)}, f32[3,16,40,4]{2,1,3,0:T(8,128)S(1)}, u32[]{:S(2)}, u32[]{:S(2)}) collective-permute-start(f32[3,16,40,4]{2,1,3,0:T(8,128)S(1)} %copy.18), channel_id=1, source_target_pairs={{0,1},{1,0},{2,3},{3,2},{4,5},{5,4},{6,7},{7,6},{8,9},{9,8},{10,11... | collective-permute-start | bytes 92168 | tf_op jit(solution)/shard_map/ppermute | solution.py:19
  22.9 2.8 %collective-permute-done.4 = f32[3,16,40,4]{2,1,3,0:T(8,128)S(1)} collective-permute-done((f32[3,16,40,4]{2,1,3,0:T(8,128)S(1)}, f32[3,16,40,4]{2,1,3,0:T(8,128)S(1)}, u32[]{:S(2)}, u32[]{:S(2)}) %collective-permute-start.4) | collective-permute-done | bytes 30752 | tf_op jit(solution)/shard_map/ppermute | solution.py:19
  26.1 1.0 collective-permute-done.5
  27.5 1.1 pad_maximum_fusion
  29.2 1.9 %fusion.6 = f32[2,14,38,134]{3,2,1,0:T(8,128)S(1)} fusion(f32[3,16,40,136]{3,2,1,0:T(8,128)S(1)} %pad_maximum_fusion, f32[14,38,134]{2,1,0:T(8,128)S(1)} %slice_add_fusion.15), kind=kLoop, calls=%fused_computation.8 | loop fusion | flops 1425760 | bytes 4847584 | tf_op jit(solution)/shard_map/div | solution.py:43
  31.1 1.9 %slice_subtract_fusion = f32[2,12,36,132]{3,2,1,0:T(8,128)S(1)} fusion(f32[3,16,40,136]{3,2,1,0:T(8,128)S(1)} %pad_maximum_fusion, f32[2,14,38,134]{3,2,1,0:T(8,128)S(1)} %fusion.6, f32[12,36,132]{2,1,0:T(8,128)S(1)} %slice_add_fusion.16), kind=kLoop, calls=%fused_computation.43 | loop fusion | flops 1254528 | bytes 4333824 | tf_op jit(solution)/shard_map/sub | solution.py:46
  33.0 1.6 %slice_subtract_fusion.1 = f32[2,10,34,130]{3,2,1,0:T(8,128)S(1)} fusion(f32[2,14,38,134]{3,2,1,0:T(8,128)S(1)} %fusion.6, f32[2,12,36,132]{3,2,1,0:T(8,128)S(1)} %slice_subtract_fusion, f32[10,34,130]{2,1,0:T(8,128)S(1)} %slice_add_fusion.17), kind=kLoop, calls=%fused_computation.53 | loop fusion | flops 972400 | bytes 3359200 | tf_op jit(solution)/shard_map/sub | solution.py:46
  35.8 2.1 %stack.65 = f32[9,8,32,128]{3,0,2,1:T(8,128)S(1)} concatenate(f32[1,8,32,128]{3,0,2,1:T(1,128)S(1)} %bitcast.249, f32[1,8,32,128]{3,0,2,1:T(1,128)S(1)} %bitcast.273, f32[1,8,32,128]{3,0,2,1:T(1,128)S(1)} %bitcast.267, f32[1,8,32,128]{3,0,2,1:T(1,128)S(1)} %bitcast.263, f32[1,8,32,128]{3,0,2,1:T(1,128)S(1)} %bitcast.261, f32[1,8,32,128]{3,0,2,1:T(1,128)S(1)} %bitcast.255, ...), dimensions={0} | concatenate | bytes 2359296 | tf_op jit(solution)/shard_map/stack | solution.py:111
  37.8 2.9 %convolution_bitcast_fusion.1 = f32[9,9]{0,1:T(8,128)S(1)} fusion(f32[9,8,32,128]{3,0,2,1:T(8,128)S(1)} %stack.65), kind=kOutput, calls=%fused_computation.14 | convolution fusion | flops 31850496 | bytes 1179972 | tf_op jit(solution)/shard_map/dot_general | solution.py:113
  40.7 1.9 %stack.75 = f32[9,32768]{1,0:T(8,128)S(1)} concatenate(f32[1,32768]{1,0:T(1,128)S(1)} %bitcast.250, f32[1,32768]{1,0:T(1,128)S(1)} %bitcast.274, f32[1,32768]{1,0:T(1,128)S(1)} %bitcast.268, f32[1,32768]{1,0:T(1,128)S(1)} %bitcast.264, f32[1,32768]{1,0:T(1,128)S(1)} %bitcast.262, f32[1,32768]{1,0:T(1,128)S(1)} %bitcast.256, f32[1,32768]{1,0:T(1,128)S(1)} %bitcast.272, ...), dimensions={0} | concatenate | bytes 2359296 | tf_op jit(solution)/shard_map/stack | solution.py:111
  42.6 2.0 %convolution_bitcast_fusion = f32[16,9]{0,1:T(8,128)S(1)} fusion(bf16[2,8,256,128]{3,2,1,0:T(8,128)(2,1)} %bitcast.275, f32[9,32768]{1,0:T(8,128)S(1)} %stack.75), kind=kOutput, calls=%fused_computation.13 | convolution fusion | flops 9732096 | bytes 2228800 | tf_op jit(solution)/shard_map/dot_general | solution.py:122
  44.7 40.0 %psum.7 = f32[25,9]{0,1:T(8,128)S(1)} all-reduce(f32[25,9]{0,1:T(8,128)S(1)} %pad_maximum_fusion.8), channel_id=1, replica_groups=mesh['gx'=4,'gy'=4,'gz'=2] {'gx','gy','gz'}, use_global_device_ids=true, to_apply=%region_0.0 | all-reduce | flops 225 | bytes 1800 | tf_op jit(solution)/shard_map/psum | solution.py:125
  102.1 2.4 %fusion = f32[1,8,32,128]{3,0,2,1:T(1,128)} fusion(f32[8,32,128,9]{2,1,0,3:T(8,128)S(1)} %bitcast.242, f32[9]{0:T(128)S(1)} %fusion.67), kind=kOutput, calls=%fused_computation | convolution fusion | flops 3538944 | bytes 1310756 | tf_op jit(solution)/shard_map/dot_general | solution.py:129
  104.5 2.4 %fusion.2 = f32[1,8,32,128]{3,0,2,1:T(1,128)} fusion(f32[8,32,128,9]{2,1,0,3:T(8,128)S(1)} %bitcast.243, f32[9]{0:T(128)S(1)} %multiply_add_fusion, f32[9]{0:T(128)S(1)} %multiply_add_fusion.1, f32[9]{0:T(128)S(1)} %select_add_fusion, f32[]{:T(128)S(6)} %div.44, f32[]{:T(128)S(6)} %div.42, f32[]{:T(128)S(6)} %div.40, f32[]{:T(128)S(6)} %div.38), kind=kOutput, calls=%fused_computation.2 | convolution fusion | flops 3539016 | bytes 1310844 | tf_op jit(solution)/shard_map/dot_general | solution.py:128
  108.3 1.1 %fusion.62 = f32[1,32768]{1,0:T(1,128)S(1)} fusion(f32[9,32768]{1,0:T(8,128)S(1)} %stack.75, f32[9]{0:T(128)S(1)} %fusion.67, f32[9]{0:T(128)S(1)} %multiply_add_fusion, f32[]{:T(128)S(6)} %div.45), kind=kOutput, calls=%fused_computation.119 | convolution fusion | flops 3538962 | bytes 1310796 | tf_op jit(solution)/shard_map/dot_general | solution.py:133
  (61 shorter events, 14.6 us)
Async XLA Ops:
  0.6 108.8 %copy-start = (f32[16,16]{1,0:T(8,128)S(1)}, f32[16,16]{1,0:T(8,128)}, u32[]{:S(2)}) copy-start(f32[16,16]{1,0:T(8,128)} %param.12) | copy-start | bytes 3076
  0.6 18.8 %copy-start.1 = (f32[8,32,128]{2,1,0:T(8,128)S(1)}, f32[8,32,128]{2,1,0:T(8,128)}, u32[]{:S(2)}) copy-start(f32[8,32,128]{2,1,0:T(8,128)} %param.8) | copy-start | bytes 393220
  0.7 18.8 %copy-start.2 = (f32[8,32,128]{2,1,0:T(8,128)S(1)}, f32[8,32,128]{2,1,0:T(8,128)}, u32[]{:S(2)}) copy-start(f32[8,32,128]{2,1,0:T(8,128)} %param.7) | copy-start | bytes 393220
  0.7 18.8 %copy-start.3 = (f32[8,32,128]{2,1,0:T(8,128)S(1)}, f32[8,32,128]{2,1,0:T(8,128)}, u32[]{:S(2)}) copy-start(f32[8,32,128]{2,1,0:T(8,128)} %param.9) | copy-start | bytes 393220
  1.8 5.8 %collective-permute-start = (f32[3,4,32,128]{3,2,1,0:T(8,128)S(1)}, f32[3,4,32,128]{3,2,1,0:T(8,128)S(1)}, u32[]{:S(2)}, u32[]{:S(2)}) collective-permute-start(f32[3,4,32,128]{3,2,1,0:T(8,128)S(1)} %get-tuple-element.13), channel_id=1, source_target_pairs={{0,8},{8,16},{16,24},{24,0},{1,9},{9,17},{17,25},{25,1},{2,10},{10... | collective-permute-start | bytes 589832 | tf_op jit(solution)/shard_map/ppermute | solution.py:19
  2.4 7.2 %collective-permute-start.1 = (f32[3,4,32,128]{3,2,1,0:T(8,128)S(1)}, f32[3,4,32,128]{3,2,1,0:T(8,128)S(1)}, u32[]{:S(2)}, u32[]{:S(2)}) collective-permute-start(f32[3,4,32,128]{3,2,1,0:T(8,128)S(1)} %get-tuple-element.14), channel_id=1, source_target_pairs={{8,0},{16,8},{24,16},{0,24},{9,1},{17,9},{25,17},{1,25},{10,2},{18... | collective-permute-start | bytes 589832 | tf_op jit(solution)/shard_map/ppermute | solution.py:22
  10.5 7.5 %collective-permute-start.2 = (f32[3,16,4,128]{3,2,1,0:T(4,128)S(1)}, f32[3,16,4,128]{3,2,1,0:T(4,128)S(1)}, u32[]{:S(2)}, u32[]{:S(2)}) collective-permute-start(f32[3,16,4,128]{3,2,1,0:T(4,128)S(1)} %get-tuple-element.11), channel_id=1, source_target_pairs={{0,2},{2,4},{4,6},{6,0},{1,3},{3,5},{5,7},{7,1},{8,10},{10,12},{12... | collective-permute-start | bytes 294920 | tf_op jit(solution)/shard_map/ppermute | solution.py:19
  12.1 7.3 %collective-permute-start.3 = (f32[3,16,4,128]{3,2,1,0:T(4,128)S(1)}, f32[3,16,4,128]{3,2,1,0:T(4,128)S(1)}, u32[]{:S(2)}, u32[]{:S(2)}) collective-permute-start(f32[3,16,4,128]{3,2,1,0:T(4,128)S(1)} %get-tuple-element.12), channel_id=1, source_target_pairs={{2,0},{4,2},{6,4},{0,6},{3,1},{5,3},{7,5},{1,7},{10,8},{12,10},{14... | collective-permute-start | bytes 294920 | tf_op jit(solution)/shard_map/ppermute | solution.py:22
  19.9 2.9 %copy-start.5 = (f32[9,9]{1,0:T(8,128)S(1)}, f32[9,9]{1,0:T(8,128)}, u32[]{:S(2)}) copy-start(f32[9,9]{1,0:T(8,128)} %constant.17.clone) | copy-start | bytes 976
  20.3 5.4 %collective-permute-start.4 = (f32[3,16,40,4]{2,1,3,0:T(8,128)S(1)}, f32[3,16,40,4]{2,1,3,0:T(8,128)S(1)}, u32[]{:S(2)}, u32[]{:S(2)}) collective-permute-start(f32[3,16,40,4]{2,1,3,0:T(8,128)S(1)} %copy.18), channel_id=1, source_target_pairs={{0,1},{1,0},{2,3},{3,2},{4,5},{5,4},{6,7},{7,6},{8,9},{9,8},{10,11... | collective-permute-start | bytes 92168 | tf_op jit(solution)/shard_map/ppermute | solution.py:19
  22.2 4.9 %collective-permute-start.5 = (f32[3,16,40,4]{2,1,3,0:T(8,128)S(1)}, f32[3,16,40,4]{2,1,3,0:T(8,128)S(1)}, u32[]{:S(2)}, u32[]{:S(2)}) collective-permute-start(f32[3,16,40,4]{2,1,3,0:T(8,128)S(1)} %copy.19), channel_id=1, source_target_pairs={{1,0},{0,1},{3,2},{2,3},{5,4},{4,5},{7,6},{6,7},{9,8},{8,9},{11,10... | collective-permute-start | bytes 92168 | tf_op jit(solution)/shard_map/ppermute | solution.py:22
  104.5 5.1 %copy-start.4 = (bf16[16,8,32,128]{3,2,1,0:T(8,128)(2,1)S(1)}, bf16[16,8,32,128]{3,2,1,0:T(8,128)(2,1)}, u32[]{:S(2)}) copy-start(bf16[16,8,32,128]{3,2,1,0:T(8,128)(2,1)} %param.10) | copy-start | bytes 3145732
where the time goes:
time: 111 us
  blocking collectives  40 us (36%)
  matrix products  19.1 us (17%)
  waiting for transfers between devices  14 us (13%)
  between operations  11.8 us (11%)
  other arithmetic  10.2 us (9%)
  starting transfers between devices  8.58 us (8%)
  local copies, waits for them, and re-layouts  7.23 us (7%)
    psum x1, blocking collectives, body(): lax.psum(jnp.concatenate([gram_block, projections], 0), ('gx', 'gy', 'gz'))  40 us
    ppermute x3, waiting for transfers between devices, extended(): lax.ppermute(lax.slice_in_dim(block, block.shape[dim] - width, None, axis...  9.69 us
    ppermute x3, starting transfers between devices, extended(): lax.ppermute(lax.slice_in_dim(block, 0, width, axis=dim), axis, backward)  4.85 us
    ppermute x3, waiting for transfers between devices, extended(): lax.ppermute(lax.slice_in_dim(block, 0, width, axis=dim), axis, backward)  4.3 us
    another operation x2, local copies, waits for them, and re-layouts, body(): basis = jnp.stack(search_basis + residue_basis)  3.93 us
    sub x3, other arithmetic, chebyshev_next(): return 2.0 * scaled - earlier  3.83 us
    dot_general x5, matrix products, coordinates(): jnp.dot(gram_block, residue, precision=precise)  3.78 us
    ppermute x3, starting transfers between devices, extended(): lax.ppermute(lax.slice_in_dim(block, block.shape[dim] - width, None, axis...  3.73 us
  transfers between devices with their start and end apart: 6, of which 6 were waited for; matrix products, arithmetic and copies ran while one was open for 1% of the time, Pallas kernels for 0%

commit v1 on v0

--- a/solution.py
+++ b/solution.py
@@ -122,7 +122,7 @@
     projections = lax.dot_general(
         images, rounded, (((1,), (1,)), ((), ())), preferred_element_type=jnp.float32
     )
-    totals = lax.psum(jnp.concatenate([gram_block, projections], 0), ("gx", "gy", "gz"))
+    totals = lax.psum(lax.psum(jnp.concatenate([gram_block, projections], 0), ("gy", "gz")), "gx")
     update, residue, search, weights = coordinates(totals, coupling_inverse)
     shape = residual.shape
     solution_delta = jnp.dot(update, basis_flat, precision=precise).reshape(shape)

time: 111 us -> 97.5 us (0.88)
  blocking collectives: 40 us -> 26.1 us
    psum x1 -> x2, blocking collectives: 40 us -> 26.1 us  [the longest x1 20.4 us: body(): lax.psum(jnp.concatenate([gram_block, projections], 0), ('gy', 'gz'))]
where the time goes in v1:
time: 97.5 us; the launch traced here: 97.1 us
  blocking collectives  26.1 us (27%)
  matrix products  19.1 us (20%)
  waiting for transfers between devices  14 us (14%)
  between operations  11.8 us (12%)
  other arithmetic  10.2 us (10%)
  starting transfers between devices  8.58 us (9%)
  local copies, waits for them, and re-layouts  7.23 us (7%)
    psum x1, blocking collectives, body(): lax.psum(jnp.concatenate([gram_block, projections], 0), ('gy', 'gz'))  20.4 us
    ppermute x3, waiting for transfers between devices, extended(): lax.ppermute(lax.slice_in_dim(block, block.shape[dim] - width, None, axis...  9.69 us
    psum x1, blocking collectives, body(): lax.psum(lax.psum(jnp.concatenate([gram_block, projections], 0), ('gy', '...  5.77 us
    ppermute x3, starting transfers between devices, extended(): lax.ppermute(lax.slice_in_dim(block, 0, width, axis=dim), axis, backward)  4.85 us
    ppermute x3, waiting for transfers between devices, extended(): lax.ppermute(lax.slice_in_dim(block, 0, width, axis=dim), axis, backward)  4.3 us
    another operation x2, local copies, waits for them, and re-layouts, body(): basis = jnp.stack(search_basis + residue_basis)  3.93 us
    sub x3, other arithmetic, chebyshev_next(): return 2.0 * scaled - earlier  3.83 us
    dot_general x5, matrix products, coordinates(): jnp.dot(gram_block, residue, precision=precise)  3.78 us
  transfers between devices with their start and end apart: 6, of which 6 were waited for; matrix products, arithmetic and copies ran while one was open for 1% of the time, Pallas kernels for 0%

profile of v1, /device:TPU:0, one launch (start us, length us, event | category | flops | bytes accessed | tf_op | source)
XLA Modules:
  0.0 97.1 jit_solution(14824524025075204334)
XLA Ops:
  0.7 1.1 %pad_maximum_fusion.2 = f32[3,8,32,128]{3,2,1,0:T(8,128)S(1)} fusion(f32[1,8,32,128]{3,2,1,0:T(8,128)} %bitcast.257, f32[1,8,32,128]{3,2,1,0:T(8,128)} %bitcast.251, f32[1,8,32,128]{3,2,1,0:T(8,128)} %bitcast.245), kind=kLoop, calls=%fused_computation.81 | loop fusion | flops 196608 | bytes 786432 | tf_op jit(solution)/shard_map/stack | solution.py:94
  2.4 2.0 %collective-permute-start.1 = (f32[3,4,32,128]{3,2,1,0:T(8,128)S(1)}, f32[3,4,32,128]{3,2,1,0:T(8,128)S(1)}, u32[]{:S(2)}, u32[]{:S(2)}) collective-permute-start(f32[3,4,32,128]{3,2,1,0:T(8,128)S(1)} %get-tuple-element.14), channel_id=1, source_target_pairs={{8,0},{16,8},{24,16},{0,24},{9,1},{17,9},{25,17},{1,25},{10,2},{18... | collective-permute-start | bytes 589832 | tf_op jit(solution)/shard_map/ppermute | solution.py:22
  4.4 3.3 %collective-permute-done = f32[3,4,32,128]{3,2,1,0:T(8,128)S(1)} collective-permute-done((f32[3,4,32,128]{3,2,1,0:T(8,128)S(1)}, f32[3,4,32,128]{3,2,1,0:T(8,128)S(1)}, u32[]{:S(2)}, u32[]{:S(2)}) %collective-permute-start) | collective-permute-done | bytes 196640 | tf_op jit(solution)/shard_map/ppermute | solution.py:19
  7.7 1.9 %collective-permute-done.1 = f32[3,4,32,128]{3,2,1,0:T(8,128)S(1)} collective-permute-done((f32[3,4,32,128]{3,2,1,0:T(8,128)S(1)}, f32[3,4,32,128]{3,2,1,0:T(8,128)S(1)}, u32[]{:S(2)}, u32[]{:S(2)}) %collective-permute-start.1) | collective-permute-done | bytes 196640 | tf_op jit(solution)/shard_map/ppermute | solution.py:22
  10.5 1.6 %collective-permute-start.2 = (f32[3,16,4,128]{3,2,1,0:T(4,128)S(1)}, f32[3,16,4,128]{3,2,1,0:T(4,128)S(1)}, u32[]{:S(2)}, u32[]{:S(2)}) collective-permute-start(f32[3,16,4,128]{3,2,1,0:T(4,128)S(1)} %get-tuple-element.11), channel_id=1, source_target_pairs={{0,2},{2,4},{4,6},{6,0},{1,3},{3,5},{5,7},{7,1},{8,10},{10,12},{12... | collective-permute-start | bytes 294920 | tf_op jit(solution)/shard_map/ppermute | solution.py:19
  12.1 2.2 %collective-permute-start.3 = (f32[3,16,4,128]{3,2,1,0:T(4,128)S(1)}, f32[3,16,4,128]{3,2,1,0:T(4,128)S(1)}, u32[]{:S(2)}, u32[]{:S(2)}) collective-permute-start(f32[3,16,4,128]{3,2,1,0:T(4,128)S(1)} %get-tuple-element.12), channel_id=1, source_target_pairs={{2,0},{4,2},{6,4},{0,6},{3,1},{5,3},{7,5},{1,7},{10,8},{12,10},{14... | collective-permute-start | bytes 294920 | tf_op jit(solution)/shard_map/ppermute | solution.py:22
  14.4 3.7 %collective-permute-done.2 = f32[3,16,4,128]{3,2,1,0:T(4,128)S(1)} collective-permute-done((f32[3,16,4,128]{3,2,1,0:T(4,128)S(1)}, f32[3,16,4,128]{3,2,1,0:T(4,128)S(1)}, u32[]{:S(2)}, u32[]{:S(2)}) %collective-permute-start.2) | collective-permute-done | bytes 98336 | tf_op jit(solution)/shard_map/ppermute | solution.py:19
  18.0 1.4 %collective-permute-done.3 = f32[3,16,4,128]{3,2,1,0:T(4,128)S(1)} collective-permute-done((f32[3,16,4,128]{3,2,1,0:T(4,128)S(1)}, f32[3,16,4,128]{3,2,1,0:T(4,128)S(1)}, u32[]{:S(2)}, u32[]{:S(2)}) %collective-permute-start.3) | collective-permute-done | bytes 98336 | tf_op jit(solution)/shard_map/ppermute | solution.py:22
  20.3 1.6 %collective-permute-start.4 = (f32[3,16,40,4]{2,1,3,0:T(8,128)S(1)}, f32[3,16,40,4]{2,1,3,0:T(8,128)S(1)}, u32[]{:S(2)}, u32[]{:S(2)}) collective-permute-start(f32[3,16,40,4]{2,1,3,0:T(8,128)S(1)} %copy.18), channel_id=1, source_target_pairs={{0,1},{1,0},{2,3},{3,2},{4,5},{5,4},{6,7},{7,6},{8,9},{9,8},{10,11... | collective-permute-start | bytes 92168 | tf_op jit(solution)/shard_map/ppermute | solution.py:19
  22.9 2.8 %collective-permute-done.4 = f32[3,16,40,4]{2,1,3,0:T(8,128)S(1)} collective-permute-done((f32[3,16,40,4]{2,1,3,0:T(8,128)S(1)}, f32[3,16,40,4]{2,1,3,0:T(8,128)S(1)}, u32[]{:S(2)}, u32[]{:S(2)}) %collective-permute-start.4) | collective-permute-done | bytes 30752 | tf_op jit(solution)/shard_map/ppermute | solution.py:19
  26.1 1.0 collective-permute-done.5
  27.5 1.1 %pad_maximum_fusion = f32[3,16,40,136]{3,2,1,0:T(8,128)S(1)} fusion(f32[3,16,40,4]{3,2,1,0:T(8,128)S(1)} %copy.21, f32[3,16,4,128]{3,2,1,0:T(4,128)S(1)} %collective-permute-done.3, f32[3,4,32,128]{3,2,1,0:T(8,128)S(1)} %collective-permute-done.1, f32[1,8,32,128]{3,2,1,0:T(8,128)S(1)} %bitcast.260, f32[1,8,32,128]{3,2,1,0:T(8,128)S(1)} %bitcast.254, ...), kind=kLoop, calls=%fused_computation.4 | loop fusion | flops 2088960 | bytes 2088960 | tf_op jit(solution)/shard_map/concatenate | solution.py:23
  29.2 1.9 %fusion.6 = f32[2,14,38,134]{3,2,1,0:T(8,128)S(1)} fusion(f32[3,16,40,136]{3,2,1,0:T(8,128)S(1)} %pad_maximum_fusion, f32[14,38,134]{2,1,0:T(8,128)S(1)} %slice_add_fusion.15), kind=kLoop, calls=%fused_computation.8 | loop fusion | flops 1425760 | bytes 4847584 | tf_op jit(solution)/shard_map/div | solution.py:43
  31.1 1.9 %slice_subtract_fusion = f32[2,12,36,132]{3,2,1,0:T(8,128)S(1)} fusion(f32[3,16,40,136]{3,2,1,0:T(8,128)S(1)} %pad_maximum_fusion, f32[2,14,38,134]{3,2,1,0:T(8,128)S(1)} %fusion.6, f32[12,36,132]{2,1,0:T(8,128)S(1)} %slice_add_fusion.16), kind=kLoop, calls=%fused_computation.43 | loop fusion | flops 1254528 | bytes 4333824 | tf_op jit(solution)/shard_map/sub | solution.py:46
  33.0 1.6 %slice_subtract_fusion.1 = f32[2,10,34,130]{3,2,1,0:T(8,128)S(1)} fusion(f32[2,14,38,134]{3,2,1,0:T(8,128)S(1)} %fusion.6, f32[2,12,36,132]{3,2,1,0:T(8,128)S(1)} %slice_subtract_fusion, f32[10,34,130]{2,1,0:T(8,128)S(1)} %slice_add_fusion.17), kind=kLoop, calls=%fused_computation.53 | loop fusion | flops 972400 | bytes 3359200 | tf_op jit(solution)/shard_map/sub | solution.py:46
  35.8 2.1 %stack.65 = f32[9,8,32,128]{3,0,2,1:T(8,128)S(1)} concatenate(f32[1,8,32,128]{3,0,2,1:T(1,128)S(1)} %bitcast.249, f32[1,8,32,128]{3,0,2,1:T(1,128)S(1)} %bitcast.273, f32[1,8,32,128]{3,0,2,1:T(1,128)S(1)} %bitcast.267, f32[1,8,32,128]{3,0,2,1:T(1,128)S(1)} %bitcast.263, f32[1,8,32,128]{3,0,2,1:T(1,128)S(1)} %bitcast.261, f32[1,8,32,128]{3,0,2,1:T(1,128)S(1)} %bitcast.255, ...), dimensions={0} | concatenate | bytes 2359296 | tf_op jit(solution)/shard_map/stack | solution.py:111
  37.8 2.9 %convolution_bitcast_fusion.1 = f32[9,9]{0,1:T(8,128)S(1)} fusion(f32[9,8,32,128]{3,0,2,1:T(8,128)S(1)} %stack.65), kind=kOutput, calls=%fused_computation.14 | convolution fusion | flops 31850496 | bytes 1179972 | tf_op jit(solution)/shard_map/dot_general | solution.py:113
  40.7 1.9 %stack.75 = f32[9,32768]{1,0:T(8,128)S(1)} concatenate(f32[1,32768]{1,0:T(1,128)S(1)} %bitcast.250, f32[1,32768]{1,0:T(1,128)S(1)} %bitcast.274, f32[1,32768]{1,0:T(1,128)S(1)} %bitcast.268, f32[1,32768]{1,0:T(1,128)S(1)} %bitcast.264, f32[1,32768]{1,0:T(1,128)S(1)} %bitcast.262, f32[1,32768]{1,0:T(1,128)S(1)} %bitcast.256, f32[1,32768]{1,0:T(1,128)S(1)} %bitcast.272, ...), dimensions={0} | concatenate | bytes 2359296 | tf_op jit(solution)/shard_map/stack | solution.py:111
  42.6 2.0 %convolution_bitcast_fusion = f32[16,9]{0,1:T(8,128)S(1)} fusion(bf16[2,8,256,128]{3,2,1,0:T(8,128)(2,1)} %bitcast.275, f32[9,32768]{1,0:T(8,128)S(1)} %stack.75), kind=kOutput, calls=%fused_computation.13 | convolution fusion | flops 9732096 | bytes 2228800 | tf_op jit(solution)/shard_map/dot_general | solution.py:122
  44.7 20.4 %psum.14 = f32[25,9]{0,1:T(8,128)S(1)} all-reduce(f32[25,9]{0,1:T(8,128)S(1)} %pad_maximum_fusion.8), channel_id=1, replica_groups=mesh['gx'=4,'gy'=4,'gz'=2] {'gy','gz'}, use_global_device_ids=true, to_apply=%region_0.0 | all-reduce | flops 225 | bytes 1800 | tf_op jit(solution)/shard_map/psum | solution.py:125
  65.1 5.8 %psum.15 = f32[25,9]{0,1:T(8,128)S(1)} all-reduce(f32[25,9]{0,1:T(8,128)S(1)} %psum.14), channel_id=1, replica_groups=mesh['gx'=4,'gy'=4,'gz'=2] {'gx'}, use_global_device_ids=true, to_apply=%region_1.0 | all-reduce | flops 225 | bytes 1800 | tf_op jit(solution)/shard_map/psum | solution.py:125
  88.3 2.4 %fusion = f32[1,8,32,128]{3,0,2,1:T(1,128)} fusion(f32[8,32,128,9]{2,1,0,3:T(8,128)S(1)} %bitcast.242, f32[9]{0:T(128)S(1)} %fusion.67), kind=kOutput, calls=%fused_computation | convolution fusion | flops 3538944 | bytes 1310756 | tf_op jit(solution)/shard_map/dot_general | solution.py:129
  90.7 2.4 %fusion.2 = f32[1,8,32,128]{3,0,2,1:T(1,128)} fusion(f32[8,32,128,9]{2,1,0,3:T(8,128)S(1)} %bitcast.243, f32[9]{0:T(128)S(1)} %multiply_add_fusion, f32[9]{0:T(128)S(1)} %multiply_add_fusion.1, f32[9]{0:T(128)S(1)} %select_add_fusion, f32[]{:T(128)S(6)} %div.44, f32[]{:T(128)S(6)} %div.42, f32[]{:T(128)S(6)} %div.40, f32[]{:T(128)S(6)} %div.38), kind=kOutput, calls=%fused_computation.2 | convolution fusion | flops 3539016 | bytes 1310844 | tf_op jit(solution)/shard_map/dot_general | solution.py:128
  94.5 1.1 %fusion.62 = f32[1,32768]{1,0:T(1,128)S(1)} fusion(f32[9,32768]{1,0:T(8,128)S(1)} %stack.75, f32[9]{0:T(128)S(1)} %fusion.67, f32[9]{0:T(128)S(1)} %multiply_add_fusion, f32[]{:T(128)S(6)} %div.45), kind=kOutput, calls=%fused_computation.119 | convolution fusion | flops 3538962 | bytes 1310796 | tf_op jit(solution)/shard_map/dot_general | solution.py:133
  (62 shorter events, 15.5 us)
Async XLA Ops:
  0.6 95.0 %copy-start = (f32[16,16]{1,0:T(8,128)S(1)}, f32[16,16]{1,0:T(8,128)}, u32[]{:S(2)}) copy-start(f32[16,16]{1,0:T(8,128)} %param.12) | copy-start | bytes 3076
  0.6 18.8 %copy-start.1 = (f32[8,32,128]{2,1,0:T(8,128)S(1)}, f32[8,32,128]{2,1,0:T(8,128)}, u32[]{:S(2)}) copy-start(f32[8,32,128]{2,1,0:T(8,128)} %param.8) | copy-start | bytes 393220
  0.7 18.8 %copy-start.2 = (f32[8,32,128]{2,1,0:T(8,128)S(1)}, f32[8,32,128]{2,1,0:T(8,128)}, u32[]{:S(2)}) copy-start(f32[8,32,128]{2,1,0:T(8,128)} %param.7) | copy-start | bytes 393220
  0.7 18.8 %copy-start.3 = (f32[8,32,128]{2,1,0:T(8,128)S(1)}, f32[8,32,128]{2,1,0:T(8,128)}, u32[]{:S(2)}) copy-start(f32[8,32,128]{2,1,0:T(8,128)} %param.9) | copy-start | bytes 393220
  1.8 5.8 %collective-permute-start = (f32[3,4,32,128]{3,2,1,0:T(8,128)S(1)}, f32[3,4,32,128]{3,2,1,0:T(8,128)S(1)}, u32[]{:S(2)}, u32[]{:S(2)}) collective-permute-start(f32[3,4,32,128]{3,2,1,0:T(8,128)S(1)} %get-tuple-element.13), channel_id=1, source_target_pairs={{0,8},{8,16},{16,24},{24,0},{1,9},{9,17},{17,25},{25,1},{2,10},{10... | collective-permute-start | bytes 589832 | tf_op jit(solution)/shard_map/ppermute | solution.py:19
  2.4 7.2 %collective-permute-start.1 = (f32[3,4,32,128]{3,2,1,0:T(8,128)S(1)}, f32[3,4,32,128]{3,2,1,0:T(8,128)S(1)}, u32[]{:S(2)}, u32[]{:S(2)}) collective-permute-start(f32[3,4,32,128]{3,2,1,0:T(8,128)S(1)} %get-tuple-element.14), channel_id=1, source_target_pairs={{8,0},{16,8},{24,16},{0,24},{9,1},{17,9},{25,17},{1,25},{10,2},{18... | collective-permute-start | bytes 589832 | tf_op jit(solution)/shard_map/ppermute | solution.py:22
  10.5 7.5 %collective-permute-start.2 = (f32[3,16,4,128]{3,2,1,0:T(4,128)S(1)}, f32[3,16,4,128]{3,2,1,0:T(4,128)S(1)}, u32[]{:S(2)}, u32[]{:S(2)}) collective-permute-start(f32[3,16,4,128]{3,2,1,0:T(4,128)S(1)} %get-tuple-element.11), channel_id=1, source_target_pairs={{0,2},{2,4},{4,6},{6,0},{1,3},{3,5},{5,7},{7,1},{8,10},{10,12},{12... | collective-permute-start | bytes 294920 | tf_op jit(solution)/shard_map/ppermute | solution.py:19
  12.1 7.3 %collective-permute-start.3 = (f32[3,16,4,128]{3,2,1,0:T(4,128)S(1)}, f32[3,16,4,128]{3,2,1,0:T(4,128)S(1)}, u32[]{:S(2)}, u32[]{:S(2)}) collective-permute-start(f32[3,16,4,128]{3,2,1,0:T(4,128)S(1)} %get-tuple-element.12), channel_id=1, source_target_pairs={{2,0},{4,2},{6,4},{0,6},{3,1},{5,3},{7,5},{1,7},{10,8},{12,10},{14... | collective-permute-start | bytes 294920 | tf_op jit(solution)/shard_map/ppermute | solution.py:22
  19.9 2.9 %copy-start.5 = (f32[9,9]{1,0:T(8,128)S(1)}, f32[9,9]{1,0:T(8,128)}, u32[]{:S(2)}) copy-start(f32[9,9]{1,0:T(8,128)} %constant.17.clone) | copy-start | bytes 976
  20.3 5.4 %collective-permute-start.4 = (f32[3,16,40,4]{2,1,3,0:T(8,128)S(1)}, f32[3,16,40,4]{2,1,3,0:T(8,128)S(1)}, u32[]{:S(2)}, u32[]{:S(2)}) collective-permute-start(f32[3,16,40,4]{2,1,3,0:T(8,128)S(1)} %copy.18), channel_id=1, source_target_pairs={{0,1},{1,0},{2,3},{3,2},{4,5},{5,4},{6,7},{7,6},{8,9},{9,8},{10,11... | collective-permute-start | bytes 92168 | tf_op jit(solution)/shard_map/ppermute | solution.py:19
  22.2 4.9 %collective-permute-start.5 = (f32[3,16,40,4]{2,1,3,0:T(8,128)S(1)}, f32[3,16,40,4]{2,1,3,0:T(8,128)S(1)}, u32[]{:S(2)}, u32[]{:S(2)}) collective-permute-start(f32[3,16,40,4]{2,1,3,0:T(8,128)S(1)} %copy.19), channel_id=1, source_target_pairs={{1,0},{0,1},{3,2},{2,3},{5,4},{4,5},{7,6},{6,7},{9,8},{8,9},{11,10... | collective-permute-start | bytes 92168 | tf_op jit(solution)/shard_map/ppermute | solution.py:22
  90.7 5.1 %copy-start.4 = (bf16[16,8,32,128]{3,2,1,0:T(8,128)(2,1)S(1)}, bf16[16,8,32,128]{3,2,1,0:T(8,128)(2,1)}, u32[]{:S(2)}) copy-start(bf16[16,8,32,128]{3,2,1,0:T(8,128)(2,1)} %param.10) | copy-start | bytes 3145732
